TPU v7x, 32 devices: a whole 2x2x4 slice. The times are simulated.
32 devices in a mesh: horizon: 8 (over z, x), batch: 4 (over y, core).
Axes of the slice: x: 2, y: 2, z: 4, core: 2. Of those that a mesh axis runs over, the one named last changes fastest.
Arguments:
- dynamics: float32 [4, 64, 48, 48], P('batch', 'horizon'), may hold values from -0.1 to 1.1
- inputs: float32 [4, 64, 48, 16], P('batch', 'horizon'), may hold values from -0.6 to 0.6
- state_cost: float32 [4, 64, 48, 48], P('batch', 'horizon'), may hold values from -1 to 1, as said below
- input_cost: float32 [4, 64, 16, 16], P('batch', 'horizon'), may hold values from -0.2 to 2.2, as said below
- drift: float32 [4, 64, 48], P('batch', 'horizon'), may hold values from -0.6 to 0.6
- target: float32 [4, 64, 48], P('batch', 'horizon'), may hold values from -6 to 6
- initial: float32 [4, 48], P('batch'), may hold values from -6 to 6
Outputs:
- hessian: float32 [4, 1024, 1024], P('batch', 'horizon')
- gradient: float32 [4, 1024], P('batch', 'horizon')
Inputs may be any that keep to these rules, and one draw needn't show every extreme that they name: `state_cost`: each 48 x 48 matrix is symmetric and positive definite. `input_cost`: each 16 x 16 matrix is symmetric and positive definite.
All inputs are finite; a program needn't handle non-finite values.
Results may differ from a plain program's by a relative error of at most 0.0003.
Values sent between devices are 32-bit elements; how exact they have to be, the bound alone decides.
No kernel may reach another device: no remote copies, remote signals or barrier semaphores. Data moves between devices by JAX's collectives and lax.ppermute only.
A program may use at most 128 MiB of HBM per device.

v0:
```python
import jax
import jax.numpy as jnp
from jax import lax
from jax.sharding import PartitionSpec as P

NX = 48
NU = 16


HI = lax.Precision.HIGHEST


def prefix(array, axis, combine, identity, reverse):
    count, mine = (lax.axis_size(axis), lax.axis_index(axis))
    everything = jax.tree.map(lambda part: lax.all_gather(part, axis), array)
    start = jax.tree.map(
        lambda part, zero: jnp.broadcast_to(jnp.asarray(zero, part.dtype), part.shape),
        array,
        identity,
    )

    def turn(k, before):
        at = count - 1 - k if reverse else k
        reached = at > mine if reverse else at < mine
        new = combine(before, jax.tree.map(lambda part: part[at], everything))
        return jax.tree.map(lambda a, b: jnp.where(reached, a, b), new, before)

    return lax.fori_loop(0, count, turn, start)


def times_mat(left, right):
    return jnp.einsum("pij,pjk->pik", left, right, precision=HI)


def trans_mat(left, right):
    return jnp.einsum("pji,pjk->pik", left, right, precision=HI)


def times_vec(left, vector):
    return jnp.einsum("pij,pj->pi", left, vector, precision=HI)


def trans_vec(left, vector):
    return jnp.einsum("pji,pj->pi", left, vector, precision=HI)


def body(dynamics, inputs, state_cost, input_cost, drift, target, initial):
    count = lax.axis_size("horizon")
    device = lax.axis_index("horizon")
    problems = inputs.shape[0]
    sections = inputs.shape[1]
    local_cols = sections * NU
    total_cols = local_cols * count
    offset_cols = device * local_cols
    eye_state = jnp.broadcast_to(jnp.eye(NX, dtype=jnp.float32), (problems, NX, NX))
    zero_square = jnp.zeros((problems, NX, NX), jnp.float32)
    zero_vector = jnp.zeros((problems, NX), jnp.float32)
    section_dynamics = jnp.moveaxis(dynamics, 1, 0)
    section_inputs = jnp.moveaxis(inputs, 1, 0)
    section_costs = jnp.moveaxis(state_cost, 1, 0)
    section_input_costs = jnp.moveaxis(input_cost, 1, 0)
    section_drift = jnp.moveaxis(drift, 1, 0)
    section_target = jnp.moveaxis(target, 1, 0)
    indices = jnp.arange(sections, dtype=jnp.int32)

    def forward_local(carry, parts):
        transfer, shift_sum = carry
        matrix, shift_vec = parts
        return ((times_mat(matrix, transfer), times_vec(matrix, shift_sum) + shift_vec), None)

    (transfer, shift_sum), _ = lax.scan(
        forward_local, (eye_state, zero_vector), (section_dynamics, section_drift)
    )

    def closing_local(tail, parts):
        matrix, weight = parts
        return (trans_mat(matrix, times_mat(weight + tail, matrix)), None)

    closing, _ = lax.scan(
        closing_local, zero_square, (section_dynamics, section_costs), reverse=True
    )

    def chain_forward(earlier, later):
        return (times_mat(later[0], earlier[0]), times_vec(later[0], earlier[1]) + later[1])

    entry_map, entry_shift = prefix(
        (transfer, shift_sum), "horizon", chain_forward, (eye_state, zero_vector), False
    )

    def chain_backward(earlier, later):
        return (
            times_mat(earlier[0], later[0]),
            trans_mat(later[0], times_mat(earlier[1], later[0])) + later[1],
        )

    _, tail_cost = prefix(
        (transfer, closing), "horizon", chain_backward, (eye_state, zero_square), True
    )
    start_state = times_vec(entry_map, initial) + entry_shift

    def roll_states(state, parts):
        matrix, shift_vec, goal, weight = parts
        after = times_vec(matrix, state) + shift_vec
        return (after, times_vec(weight, after - goal))

    _, weighted = lax.scan(
        roll_states, start_state, (section_dynamics, section_drift, section_target, section_costs)
    )

    def sweep_costs(tail, parts):
        matrix, weight = parts
        total_cost = weight + tail
        return (trans_mat(matrix, times_mat(total_cost, matrix)), total_cost)

    _, cost_to_go = lax.scan(
        sweep_costs, tail_cost, (section_dynamics, section_costs), reverse=True
    )
    value_cols = jnp.einsum("spij,spjk->spik", cost_to_go, section_inputs, precision=HI)

    def sweep_compact(carry, parts):
        block, vector = carry
        matrix, value, weight, index = parts
        placed = lax.dynamic_update_slice_in_dim(block, value, index * NU, 2)
        return ((trans_mat(matrix, placed), trans_vec(matrix, weight + vector)), (block, vector))

    compact_start = (jnp.zeros((problems, NX, local_cols), jnp.float32), zero_vector)
    (local_block, local_vector), (later_blocks, later_vectors) = lax.scan(
        sweep_compact,
        compact_start,
        (section_dynamics, value_cols, weighted, indices),
        reverse=True,
    )
    all_maps, all_blocks, all_vectors = (
        lax.all_gather(transfer[None], "horizon", axis=0, tiled=True),
        lax.all_gather(local_block[None], "horizon", axis=0, tiled=True),
        lax.all_gather(local_vector[None], "horizon", axis=0, tiled=True),
    )

    def fold_columns(carry, parts):
        product, vector = carry
        matrix, block, piece_vector, index = parts
        active = index > device
        column_part = jnp.where(active, trans_mat(product, block), 0.0)
        vector = vector + jnp.where(active, trans_vec(product, piece_vector), 0.0)
        product = jnp.where(active, times_mat(matrix, product), product)
        return ((product, vector), column_part)

    device_ids = jnp.arange(count, dtype=jnp.int32)
    (_, incoming_vec), column_parts = lax.scan(
        fold_columns, (eye_state, zero_vector), (all_maps, all_blocks, all_vectors, device_ids)
    )
    incoming = jnp.transpose(column_parts, (1, 2, 0, 3)).reshape(problems, NX, total_cols)

    def sweep_rows(carry, parts):
        block, vector = carry
        matrix, control, later_block, later_vector, weight = parts
        row_block = trans_mat(control, block)
        row_block = lax.dynamic_update_slice_in_dim(
            row_block, trans_mat(control, later_block), offset_cols, 2
        )
        grad_block = trans_vec(control, weight + later_vector + vector)
        return ((trans_mat(matrix, block), trans_vec(matrix, vector)), (row_block, grad_block))

    _, (row_blocks, grad_blocks) = lax.scan(
        sweep_rows,
        (incoming, incoming_vec),
        (section_dynamics, section_inputs, later_blocks, later_vectors, weighted),
        reverse=True,
    )
    upper = jnp.moveaxis(row_blocks, 0, 1).reshape(problems, local_cols, total_cols)
    gradient = jnp.moveaxis(grad_blocks, 0, 1).reshape(problems, local_cols)
    received = lax.all_to_all(upper, "horizon", split_axis=2, concat_axis=2, tiled=True)
    mirrored = jnp.transpose(
        received.reshape(problems, local_cols, count, local_cols), (0, 3, 2, 1)
    ).reshape(problems, local_cols, total_cols)
    diagonal_blocks = (
        jnp.einsum("spji,spjk->spik", section_inputs, value_cols, precision=HI)
        + section_input_costs
    )
    block_diag = jnp.einsum(
        "st,spij->psitj", jnp.eye(sections, dtype=jnp.float32), diagonal_blocks, precision=HI
    ).reshape(problems, local_cols, local_cols)
    hessian = upper + mirrored
    own_tile = lax.dynamic_slice_in_dim(hessian, offset_cols, local_cols, 2) + block_diag
    hessian = lax.dynamic_update_slice_in_dim(hessian, own_tile, offset_cols, 2)
    return (hessian, gradient)


def solution(mesh):
    in_specs = (
        P("batch", "horizon", None, None),
        P("batch", "horizon", None, None),
        P("batch", "horizon", None, None),
        P("batch", "horizon", None, None),
        P("batch", "horizon", None),
        P("batch", "horizon", None),
        P("batch", None),
    )
    out_specs = (P("batch", "horizon", None), P("batch", "horizon"))
    return jax.shard_map(body, mesh=mesh, in_specs=in_specs, out_specs=out_specs, check_vma=False)
```

profile of v0, /device:TPU:0, one launch (start us, length us, event | category | flops | bytes accessed | tf_op | source)
XLA Modules:
  0.0 231.4 jit_solution(3234112378326604978)
XLA Ops:
  1.3 14.6 %while.141 = (s32[]{:T(128)}, f32[1,48,48]{2,1,0:T(8,128)S(1)}, f32[1,48]{1,0:T(1,128)S(1)}, f32[8,1,48,48]{3,2,1,0:T(8,128)}, f32[8,1,48]{2,1,0:T(1,128)}, /*index=5*/s32[]{:T(128)}) while((s32[]{:T(128)}, f32[1,48,48]{2,1,0:T(8,128)S(1)}, f32[1,48]{1,0:T(1,128)S(1)}, f32[8,1,48,48]{3,2,1,0:T(8,128)}, f32[8,1,48]{2,1,0:T(1,128)}, ...), condition=%wide.region_1.2_spmd, body=%wide.region_0.1_spmd.sunk | while | flops 1354802 | bytes 88901 | solution.py:71
  2.2 0.9 convolution_bitcast_fusion.22
  4.0 0.9 convolution_bitcast_fusion.22
  5.8 0.9 convolution_bitcast_fusion.22
  7.6 0.9 convolution_bitcast_fusion.22
  11.3 0.9 convolution_bitcast_fusion.22
  13.1 0.9 convolution_bitcast_fusion.22
  15.0 0.9 convolution_bitcast_fusion.22
  15.9 32.6 %all-gather = f32[8,48,48]{2,1,0:T(8,128)S(1)} all-gather(f32[1,48,48]{2,1,0:T(8,128)S(1)} %get-tuple-element.948), channel_id=2, replica_groups=mesh['horizon'=8,'batch'=4] {'horizon'}, dimensions={0}, use_global_device_ids=true | all-gather | bytes 82944 | tf_op jit(solution)/shard_map/all_gather | solution.py:134
  48.5 20.5 %all-gather.5 = f32[8,1,48]{2,1,0:T(1,128)S(1)} all-gather(f32[1,1,48]{2,1,0:T(1,128)S(1)} %bitcast.502), channel_id=4, replica_groups=mesh['horizon'=8,'batch'=4] {'horizon'}, dimensions={0}, use_global_device_ids=true | all-gather | bytes 1728 | tf_op jit(solution)/shard_map/all_gather | solution.py:15
  68.9 2.9 %while.148 = (s32[]{:T(128)}, f32[1,48,48]{2,1,0:T(8,128)S(1)}, f32[1,48]{1,0:T(1,128)S(1)}, s32[]{:T(128)}, f32[8,1,48,48]{3,2,1,0:T(8,128)S(1)}, /*index=5*/f32[8,1,48]{2,1,0:T(1,128)S(1)}, s32[]{:T(128)}, s32[]{:T(128)}) while((s32[]{:T(128)}, f32[1,48,48]{2,1,0:T(8,128)S(1)}, f32[1,48]{1,0:T(1,128)S(1)}, s32[]{:T(128)}, ...), condition=%wide.region_9.10_spmd.clone, body=%wide.region_8.9_spmd.clone.sunk | while | flops 1357252 | bytes 130732 | solution.py:28
  72.0 13.1 %while.144 = (s32[]{:T(128)}, f32[1,48]{1,0:T(1,128)S(1)}, f32[8,1,48]{2,1,0:T(1,128)S(1)}, f32[8,1,48,48]{3,2,1,0:T(8,128)S(1)}, f32[8,1,48]{2,1,0:T(1,128)}, /...) while((s32[]{:T(128)}, f32[1,48]{1,0:T(1,128)S(1)}, f32[8,1,48]{2,1,0:T(1,128)S(1)}, ...), condition=%wide.region_11.12_spmd, body=%wide.region_10.11_spmd.sunk | while | flops 55394 | bytes 54933 | solution.py:106
  85.2 3.3 %while.142 = (s32[]{:T(128)}, f32[1,48,48]{2,1,0:T(8,128)S(1)}, f32[8,1,48,48]{3,2,1,0:T(8,128)S(1)}, f32[8,1,48,48]{3,2,1,0:T(8,128)S(1)}, s32[]{:T(128)}, /*index=5*/s32[]{:T(128)}) while((s32[]{:T(128)}, f32[1,48,48]{2,1,0:T(8,128)S(1)}, f32[8,1,48,48]{3,2,1,0:T(8,128)S(1)}, f32[8,1,48,48]{3,2,1,0:T(8,128)S(1)}, s32[]{:T(128)}, ...), condition=%wide.region_3.4_spmd, body=%wide.region_2.3_spmd.sunk | while | flops 2656515 | bytes 142421 | solution.py:79
  88.5 30.6 %all-gather.1 = f32[8,48,48]{2,1,0:T(8,128)S(1)} all-gather(f32[1,48,48]{2,1,0:T(8,128)S(1)} %get-tuple-element.949), channel_id=3, replica_groups=mesh['horizon'=8,'batch'=4] {'horizon'}, dimensions={0}, use_global_device_ids=true | all-gather | bytes 82944 | tf_op jit(solution)/shard_map/all_gather | solution.py:15
  119.2 4.0 %while.147 = (s32[]{:T(128)}, f32[1,48,48]{2,1,0:T(8,128)S(1)}, s32[]{:T(128)}, f32[8,1,48,48]{3,2,1,0:T(8,128)S(1)}, f32[8,1,48,48]{3,2,1,0:T(8,128)S(1)}, /*index=5*/s32[]{:T(128)}, s32[]{:T(128)}, s32[]{:T(128)}, s32[]{:T(128)}) while((s32[]{:T(128)}, f32[1,48,48]{2,1,0:T(8,128)S(1)}, s32[]{:T(128)}, ...), condition=%wide.region_5.6_spmd.clone, body=%wide.region_4.5_spmd.clone.sunk | while | flops 2663432 | bytes 168098 | solution.py:28
  123.3 3.4 %while.143 = (s32[]{:T(128)}, f32[1,48,48]{2,1,0:T(8,128)S(1)}, f32[8,1,48,48]{3,2,1,0:T(8,128)S(1)}, f32[8,1,48,48]{3,2,1,0:T(8,128)S(1)}, f32[8,1,48,48]{3,2,1,0:T(8,128)S(1)}, /*index=5*/s32[]{:T(128)}, s32[]{:T(128)}) while((s32[]{:T(128)}, f32[1,48,48]{2,1,0:T(8,128)S(1)}, f32[8,1,48,48]{3,2,1,0:T(8,128)S(1)}, ...), condition=%wide.region_7.8_spmd, body=%wide.region_6.7_spmd.sunk | while | flops 2658819 | bytes 216161 | solution.py:115
  127.2 16.6 %while.145 = (s32[]{:T(128)}, f32[1,48,128]{2,1,0:T(8,128)S(1)}, f32[1,48]{1,0:T(1,128)S(1)}, f32[8,1,48,128]{3,2,1,0:T(8,128)S(1)}, f32[8,1,48]{2,1,0:T(1,128)S...) while((s32[]{:T(128)}, f32[1,48,128]{2,1,0:T(8,128)S(1)}, ...), condition=%wide.region_13.14_spmd, body=%wide.region_12.13_spmd.sunk | while | flops 3566647 | bytes 218911 | solution.py:127
  143.9 30.8 %all-gather.4 = f32[8,48,128]{2,1,0:T(8,128)S(1)} all-gather(f32[1,48,128]{2,1,0:T(8,128)S(1)} %get-tuple-element.957), channel_id=6, replica_groups=mesh['horizon'=8,'batch'=4] {'horizon'}, dimensions={0}, use_global_device_ids=true | all-gather | bytes 221184 | tf_op jit(solution)/shard_map/all_gather | solution.py:135
  174.6 16.3 %all-gather.6 = f32[8,1,48]{2,1,0:T(1,128)S(1)} all-gather(f32[1,1,48]{2,1,0:T(1,128)S(1)} %bitcast.501), channel_id=5, replica_groups=mesh['horizon'=8,'batch'=4] {'horizon'}, dimensions={0}, use_global_device_ids=true | all-gather | bytes 1728 | tf_op jit(solution)/shard_map/all_gather | solution.py:136
  190.9 15.5 %while.149 = (s32[]{:T(128)}, f32[1,48,48]{2,1,0:T(8,128)S(1)}, f32[1,48]{1,0:T(1,128)S(1)}, f32[8,1,48,128]{3,0,1,2:T(8,128)S(1)}, s32[8]{0:T(128)S(1)}, /*inde...) while((s32[]{:T(128)}, f32[1,48,48]{2,1,0:T(8,128)S(1)}, ...), condition=%wide.region_15.16_spmd.clone, body=%wide.region_14.15_spmd.clone.sunk | while | flops 4902292 | bytes 250207 | solution.py:149
  206.5 8.8 %while.146 = (s32[]{:T(128)}, f32[1,48,1024]{2,1,0:T(8,128)S(1)}, f32[1,48]{1,0:T(1,128)S(1)}, f32[8,1,16,1024]{3,2,1,0:T(8,128)S(1)}, f32[8,1,16]{2,1,0:T(1,128...) while((s32[]{:T(128)}, f32[1,48,1024]{2,1,0:T(8,128)S(1)}, ...), condition=%wide.region_17.18_spmd, body=%wide.region_16.17_spmd.sunk | while | flops 38965344 | bytes 1291997 | solution.py:164
  215.2 1.0 copy.40
  216.3 3.6 %all-to-all-start = ((f32[1,128,1024]{1,0,2:T(1,128)}), f32[1,128,1024]{1,0,2:T(1,128)S(1)}, u32[]{:S(2)}, u32[]{:S(2)}) async-start(f32[1,128,1024]{1,0,2:T(1,128)} %copy.40), calls=%async_computation | async-start | bytes 1048576 | tf_op jit(solution)/shard_map/all_to_all | solution.py:172
  222.4 7.7 %all-to-all-done = f32[1,128,1024]{1,0,2:T(1,128)S(1)} async-done(((f32[1,128,1024]{1,0,2:T(1,128)}), f32[1,128,1024]{1,0,2:T(1,128)S(1)}, u32[]{:S(2)}, u32[]{:S(2)}) %all-to-all-start) | async-done | bytes 524320 | tf_op jit(solution)/shard_map/all_to_all | solution.py:172
  (381 shorter events, 68.5 us)
Async XLA Ops:
  0.6 71.2 %copy-start = (f32[1,48]{1,0:T(1,128)S(1)}, f32[1,48]{1,0:T(1,128)}, u32[]{:S(2)}) copy-start(f32[1,48]{1,0:T(1,128)} %param.31) | copy-start | bytes 580
  0.7 0.6 copy-start.2
  15.9 53.1 %copy-start.4 = (f32[1,48,48]{2,1,0:T(8,128)S(1)}, f32[1,48,48]{2,1,0:T(8,128)}, u32[]{:S(2)}) copy-start(f32[1,48,48]{2,1,0:T(8,128)} %copy-done.2) | copy-start | bytes 27652
  15.9 56.1 %copy-start.5 = (f32[1,8,48,48]{3,2,1,0:T(8,128)S(1)}, f32[1,8,48,48]{3,2,1,0:T(8,128)}, u32[]{:S(2)}) copy-start(f32[1,8,48,48]{3,2,1,0:T(8,128)} %param.27) | copy-start | bytes 221188
  68.9 3.1 %copy-start.1 = (f32[8,1,48,48]{3,2,1,0:T(8,128)S(1)}, f32[8,1,48,48]{3,2,1,0:T(8,128)}, u32[]{:S(2)}) copy-start(f32[8,1,48,48]{3,2,1,0:T(8,128)} %get-tuple-element.1887) | copy-start | bytes 221188
  123.2 3.5 %copy-start.6 = (f32[1,8,48,16]{2,3,1,0:T(8,128)S(1)}, f32[1,8,48,16]{2,3,1,0:T(8,128)}, u32[]{:S(2)}) copy-start(f32[1,8,48,16]{2,3,1,0:T(8,128)} %param.26) | copy-start | bytes 73732
  143.8 47.0 %copy-start.3 = (f32[1,48,48]{2,1,0:T(8,128)S(1)}, f32[1,48,48]{2,1,0:T(8,128)}, u32[]{:S(2)}) copy-start(f32[1,48,48]{2,1,0:T(8,128)} %copy-done.2) | copy-start | bytes 27652
  216.3 3.6 %copy-start.8 = (f32[1,8,16,16]{3,2,1,0:T(8,128)S(1)}, f32[1,8,16,16]{3,2,1,0:T(8,128)}, u32[]{:S(2)}) copy-start(f32[1,8,16,16]{3,2,1,0:T(8,128)} %param.28) | copy-start | bytes 24580
  216.3 13.8 %all-to-all-start = ((f32[1,128,1024]{1,0,2:T(1,128)}), f32[1,128,1024]{1,0,2:T(1,128)S(1)}, u32[]{:S(2)}, u32[]{:S(2)}) async-start(f32[1,128,1024]{1,0,2:T(1,128)} %copy.40), calls=%async_computation | async-start | bytes 1048576 | tf_op jit(solution)/shard_map/all_to_all | solution.py:172
  230.6 0.8 copy-start.7
where the time goes:
time: 233 us; the launch traced here: 231 us
  blocking collectives  131 us (56%)
  matrix products  55.7 us (24%)
  local copies, waits for them, and re-layouts  19.1 us (8%)
  loops' own time  12.6 us (5%)
  waiting for transfers between devices  7.71 us (3%)
  starting transfers between devices  3.63 us (2%)
    all_gather x2, blocking collectives, prefix(): everything = jax.tree.map(lambda part: lax.all_gather(part, axis), array)  51.1 us
    all_gather x1, blocking collectives, body(): lax.all_gather(transfer[None], 'horizon', axis=0, tiled=True)  32.6 us
    all_gather x1, blocking collectives, body(): lax.all_gather(local_block[None], 'horizon', axis=0, tiled=True)  30.8 us
    dot_general x33, matrix products, times_vec(): return jnp.einsum('pij,pj->pi', left, vector, precision=HI)  21.5 us
    all_gather x1, blocking collectives, body(): lax.all_gather(local_vector[None], 'horizon', axis=0, tiled=True)  16.3 us
    dot_general x64, matrix products, trans_mat(): return jnp.einsum('pji,pjk->pik', left, right, precision=HI)  15.1 us
    dot_general x48, matrix products, times_mat(): return jnp.einsum('pij,pjk->pik', left, right, precision=HI)  14 us
    dynamic_slice x32, local copies, waits for them, and re-layouts, body(): lax.scan(sweep_compact, compact_start, (section_dynamics, value_cols, wei...  10.1 us
  transfers between devices with their start and end apart: 1, of which 1 were waited for; matrix products, arithmetic and copies ran while one was open for 1% of the time, Pallas kernels for 0%

commit v1 on v0

v1 whole, which is shorter than its diff:
```python
import functools

import jax
import jax.numpy as jnp
from jax import lax
from jax.experimental import pallas as pl
from jax.experimental.pallas import tpu as pltpu
from jax.sharding import PartitionSpec as P

LANES = 128
HALF = 64


def split(x):
    high = x.astype(jnp.bfloat16)
    return high, (x - high.astype(jnp.float32)).astype(jnp.bfloat16)


def product(left, right, trans=False):
    dims = (((0 if trans else 1,), (0,)), ((), ()))
    mul = functools.partial(
        lax.dot_general, dimension_numbers=dims, preferred_element_type=jnp.float32
    )
    (lh, ll), (rh, rl) = split(left), split(right)
    return mul(lh, rh) + (mul(lh, rl) + mul(ll, rh))


def iota(shape, dim):
    return lax.broadcasted_iota(jnp.int32, shape, dim)


def spread(blocks, rows_of):
    total, n = blocks.shape
    width = total // rows_of * n
    copies = (iota((n, width), 1) % n == iota((n, width), 0)).astype(jnp.float32)
    wide = product(blocks, copies)
    shape = (total, width)
    return jnp.where(iota(shape, 0) // rows_of == iota(shape, 1) // n, wide, 0.0)


def respond(first, last, start):
    if last - first == 1:
        return [start[first]]
    middle = (first + last) // 2
    left, right = respond(first, middle, start), respond(middle, last, start)
    nx = left[0].shape[0]
    cols = left[0].shape[1]
    maps = [x[:, cols - LANES : cols - LANES + nx] for x in right]
    through = product(jnp.concatenate(maps, 0), left[-1])
    keep = (iota((nx, cols), 1) < cols - LANES) | (iota((nx, cols), 1) >= cols - LANES + nx)
    return left + [
        through[i * nx : (i + 1) * nx] + jnp.where(keep, x, 0.0) for i, x in enumerate(right)
    ]


def local_kernel(a_ref, b_ref, q_ref, r_ref, f_ref, g_ref, pay_ref, own_ref, row_ref):
    problems, sections, nx, nu = b_ref.shape
    cols = sections * nu
    for p in range(problems):
        placed = spread(jnp.concatenate([b_ref[p, s] for s in range(sections)], 0), nx)
        drift = f_ref[p].T
        target = g_ref[p].T
        pad = jnp.zeros((nx, LANES - nx - 1), jnp.float32)
        start = [
            jnp.concatenate(
                [
                    placed[s * nx : (s + 1) * nx],
                    jnp.concatenate([a_ref[p, s], drift[:, s : s + 1], pad], 1),
                ],
                1,
            )
            for s in range(sections)
        ]
        states = respond(0, sections, start)
        lane = iota((nx, cols + LANES), 1)
        errors = [
            jnp.where(lane == cols + nx, x - target[:, s : s + 1], x)
            for s, x in enumerate(states)
        ]
        weighted = [product(q_ref[p, s], e) for s, e in enumerate(errors)]
        square = product(
            jnp.concatenate(errors, 0), jnp.concatenate(weighted, 0), trans=True
        )
        own_ref[p] = square[:cols, :cols] + spread(
            r_ref[p].reshape(sections * nu, nu), nu
        )
        row_ref[p] = square[cols + nx : cols + nx + 1, :cols]
        end = states[-1]
        pay_ref[p, :, :cols] = square[cols : cols + nx, :cols]
        pay_ref[p, :, cols : 2 * cols] = end[:, :cols]
        pay_ref[p, :, 2 * cols :] = jnp.concatenate(
            [end[:, cols : cols + HALF], square[cols : cols + nx, cols : cols + HALF]], 1
        )


def join_kernel(count, *refs):
    pays, (own_ref, row_ref, x_ref, h_ref, grad_ref) = refs[:count], refs[count:]
    device = lax.axis_index("horizon")
    problems, cols, _ = own_ref.shape
    nx = x_ref.shape[-1]
    for p in range(problems):
        gain = lambda k: pays[k][p, :, :cols]
        reach = lambda k: pays[k][p, :, cols : 2 * cols]
        maps = [pays[k][p, :, 2 * cols : 2 * cols + HALF] for k in range(count)]
        costs = [pays[k][p, :, 2 * cols + HALF :] for k in range(count)]
        upper = [device + k < count for k in range(count)]
        moved = [None, reach(0)]
        for k in range(1, count):
            moved[k] = jnp.where(upper[k], moved[k], 0.0)
            if k + 1 < count:
                moved.append(product(maps[k][:, :nx], moved[k]))
        last = iota((HALF, cols), 0) >= nx
        costate = jnp.zeros((HALF, cols), jnp.float32)
        above = [None] * count
        for k in reversed(range(1, count)):
            above[k] = costate[:nx]
            costate = (
                product(costs[k], moved[k], True)
                + product(maps[k], costate[:nx], True)
                + jnp.where(last, costate, 0.0)
            )
        own_at = pl.multiple_of(device * cols, cols)
        h_ref[p, :, pl.ds(own_at, cols)] = own_ref[p] + product(costate[:nx], reach(0), True)
        pad = jnp.zeros((HALF - nx - 1, cols), jnp.float32)
        costate = (
            jnp.concatenate([gain(0), row_ref[p], pad], 0)
            + product(maps[0], costate[:nx], True)
            + jnp.where(last, costate, 0.0)
        )
        for k in reversed(range(1, count)):
            at = pl.multiple_of(lax.rem(device + k, count) * cols, cols)
            left = jnp.concatenate(
                [moved[k], jnp.where(upper[k], above[k], costate[:nx])], 0
            )
            right = jnp.concatenate([gain(k), reach(k)], 0)
            h_ref[p, :, pl.ds(at, cols)] = product(left, right, True)
            costate = jnp.where(
                upper[k],
                costate,
                product(maps[k], costate[:nx], True) + jnp.where(last, costate, 0.0),
            )
        grad_ref[pl.ds(p, 1), :] = product(x_ref[pl.ds(p, 1), :], costate[:nx]) + costate[nx : nx + 1]


def body(dynamics, inputs, state_cost, input_cost, drift, target, initial):
    count = lax.axis_size("horizon")
    problems, sections, nx, nu = inputs.shape
    cols = sections * nu
    f32 = jnp.float32
    pay, own, row = pl.pallas_call(
        local_kernel,
        out_shape=(
            jax.ShapeDtypeStruct((problems, nx, 2 * cols + LANES), f32),
            jax.ShapeDtypeStruct((problems, cols, cols), f32),
            jax.ShapeDtypeStruct((problems, 1, cols), f32),
        ),
        name="local",
    )(dynamics, inputs, state_cost, input_cost, drift, target)
    pays = [pay] + [
        lax.ppermute(pay, "horizon", [((i + k) % count, i) for i in range(count)])
        for k in range(1, count)
    ]
    return pl.pallas_call(
        functools.partial(join_kernel, count),
        out_shape=(
            jax.ShapeDtypeStruct((problems, cols, count * cols), f32),
            jax.ShapeDtypeStruct((problems, cols), f32),
        ),
        name="join",
    )(*pays, own, row, initial)


def solution(mesh):
    in_specs = (
        P("batch", "horizon", None, None),
        P("batch", "horizon", None, None),
        P("batch", "horizon", None, None),
        P("batch", "horizon", None, None),
        P("batch", "horizon", None),
        P("batch", "horizon", None),
        P("batch", None),
    )
    out_specs = (P("batch", "horizon", None), P("batch", "horizon"))
    return jax.shard_map(body, mesh=mesh, in_specs=in_specs, out_specs=out_specs, check_vma=False)
```

time: 233 us -> 30.4 us (0.13)
  the two profiles are of different devices: /device:TPU:0 before, /device:TPU:22 now
where the time goes in v1:
time: 30.4 us; the launch traced here: 30.2 us
  waiting for transfers between devices  10.9 us (36%)
  Pallas kernels  8.57 us (28%)
  starting transfers between devices  7.74 us (25%)
  local copies, waits for them, and re-layouts  2.24 us (7%)
  between operations  0.71 us (2%)
    ppermute x7, waiting for transfers between devices, body(): lax.ppermute(pay, 'horizon', [((i + k) % count, i) for i in range(count)])  10.9 us
    ppermute x7, starting transfers between devices, body(): lax.ppermute(pay, 'horizon', [((i + k) % count, i) for i in range(count)])  7.74 us
    pallas_call x1, Pallas kernels, body(): pl.pallas_call(functools.partial(join_kernel, count), out_shape=(jax.Shap...  5.14 us
    pallas_call x1, Pallas kernels, body(): pl.pallas_call(local_kernel, out_shape=(jax.ShapeDtypeStruct((problems, n...  3.43 us
    unnamed x15, local copies, waits for them, and re-layouts  2.24 us
  transfers between devices with their start and end apart: 7, of which 3 were waited for; matrix products, arithmetic and copies ran while one was open for 0% of the time, Pallas kernels for 0%

profile of v1, /device:TPU:22, one launch (start us, length us, event | category | flops | bytes accessed | tf_op | source)
XLA Modules:
  0.0 30.2 jit_solution(13223551388272488835)
XLA Ops:
  0.6 1.6 %copy.9.b_ref = f32[1,8,48,16]{3,2,1,0:T(8,128)} copy(f32[1,8,48,16]{2,3,1,0:T(8,128)} %param.8) | data formatting | bytes 49152 | tf_op args[1]
  2.3 3.4 %local.1 = (f32[1,48,384]{2,1,0:T(8,128)}, f32[1,128,128]{2,1,0:T(8,128)}, f32[1,1,128]{2,1,0:T(1,128)}) custom-call(f32[1,8,48,48]{3,2,1,0:T(8,128)} %a_ref.1, f32[1,8,48,16]{3,2,1,0:T(8,128)} %copy.9.b_ref, f32[1,8,48,48]{3,2,1,0:T(8,128)} %q_ref.1, f32[1,8,16,16]{3,2,1,0:T(8,128)} %r_ref.1, f32[1,8,48]{2,1,0:T(8,128)} %f_ref.1, f32[1,8,48]{2,1,0:T(8,128)} %g_ref.1), custom_call_target="tpu_custom_call" | custom-call | tf_op jit(solution)/shard_map/local/pallas_call | solution.py:150
  5.7 1.6 %collective-permute-start.6 = (f32[1,48,384]{2,1,0:T(8,128)}, f32[1,48,384]{2,1,0:T(8,128)S(1)}, u32[]{:S(2)}, u32[]{:S(2)}) collective-permute-start(f32[1,48,384]{2,1,0:T(8,128)} %get-tuple-element.5.refs_0_), channel_id=1, source_target_pairs={{28,0},{0,4},{4,8},{8,12},{12,16},{16,20},{20,24},{24,28},{29,1},{... | collective-permute-start | bytes 221192 | tf_op jit(solution)/shard_map/ppermute | solution.py:160
  7.2 0.2 collective-permute-start.5
  7.5 1.6 %collective-permute-start.4 = (f32[1,48,384]{2,1,0:T(8,128)}, f32[1,48,384]{2,1,0:T(8,128)S(1)}, u32[]{:S(2)}, u32[]{:S(2)}) collective-permute-start(f32[1,48,384]{2,1,0:T(8,128)} %get-tuple-element.5.refs_0_), channel_id=1, source_target_pairs={{20,0},{24,4},{28,8},{0,12},{4,16},{8,20},{12,24},{16,28},{21,1},{... | collective-permute-start | bytes 221192 | tf_op jit(solution)/shard_map/ppermute | solution.py:160
  9.1 2.6 %collective-permute-start.3 = (f32[1,48,384]{2,1,0:T(8,128)}, f32[1,48,384]{2,1,0:T(8,128)S(1)}, u32[]{:S(2)}, u32[]{:S(2)}) collective-permute-start(f32[1,48,384]{2,1,0:T(8,128)} %get-tuple-element.5.refs_0_), channel_id=1, source_target_pairs={{16,0},{20,4},{24,8},{28,12},{0,16},{4,20},{8,24},{12,28},{17,1},{... | collective-permute-start | bytes 221192 | tf_op jit(solution)/shard_map/ppermute | solution.py:160
  11.7 1.3 %collective-permute-start.2 = (f32[1,48,384]{2,1,0:T(8,128)}, f32[1,48,384]{2,1,0:T(8,128)S(1)}, u32[]{:S(2)}, u32[]{:S(2)}) collective-permute-start(f32[1,48,384]{2,1,0:T(8,128)} %get-tuple-element.5.refs_0_), channel_id=1, source_target_pairs={{12,0},{16,4},{20,8},{24,12},{28,16},{0,20},{4,24},{8,28},{13,1},{... | collective-permute-start | bytes 221192 | tf_op jit(solution)/shard_map/ppermute | solution.py:160
  13.0 0.0 collective-permute-done.6.refs_7_
  13.0 0.4 %collective-permute-start.1 = (f32[1,48,384]{2,1,0:T(8,128)}, f32[1,48,384]{2,1,0:T(8,128)S(1)}, u32[]{:S(2)}, u32[]{:S(2)}) collective-permute-start(f32[1,48,384]{2,1,0:T(8,128)} %get-tuple-element.5.refs_0_), channel_id=1, source_target_pairs={{8,0},{12,4},{16,8},{20,12},{24,16},{28,20},{0,24},{4,28},{9,1},{1... | collective-permute-start | bytes 221192 | tf_op jit(solution)/shard_map/ppermute | solution.py:160
  13.4 5.5 %collective-permute-done.5.refs_6_ = f32[1,48,384]{2,1,0:T(8,128)S(1)} collective-permute-done((f32[1,48,384]{2,1,0:T(8,128)}, f32[1,48,384]{2,1,0:T(8,128)S(1)}, u32[]{:S(2)}, u32[]{:S(2)}) %collective-permute-start.5) | collective-permute-done | bytes 73760 | tf_op jit(solution)/shard_map/ppermute | solution.py:160
  18.9 0.0 collective-permute-start
  18.9 0.0 collective-permute-done.4.refs_5_
  18.9 0.0 copy-start.2
  18.9 0.0 collective-permute-done.3.refs_4_
  18.9 0.0 copy-start.3
  19.0 0.0 collective-permute-done.2.refs_3_
  19.0 0.0 copy-start.4
  19.0 1.2 %collective-permute-done.1.refs_2_ = f32[1,48,384]{2,1,0:T(8,128)S(1)} collective-permute-done((f32[1,48,384]{2,1,0:T(8,128)}, f32[1,48,384]{2,1,0:T(8,128)S(1)}, u32[]{:S(2)}, u32[]{:S(2)}) %collective-permute-start.1) | collective-permute-done | bytes 73760 | tf_op jit(solution)/shard_map/ppermute | solution.py:160
  20.2 4.2 %collective-permute-done.refs_1_ = f32[1,48,384]{2,1,0:T(8,128)S(1)} collective-permute-done((f32[1,48,384]{2,1,0:T(8,128)}, f32[1,48,384]{2,1,0:T(8,128)S(1)}, u32[]{:S(2)}, u32[]{:S(2)}) %collective-permute-start) | collective-permute-done | bytes 73760 | tf_op jit(solution)/shard_map/ppermute | solution.py:160
  24.4 0.0 copy-done
  24.4 0.0 copy-done.1
  24.4 0.0 copy-done.2
  24.4 0.6 %copy-done.6 = f32[1,48,384]{2,1,0:T(8,128)} copy-done((f32[1,48,384]{2,1,0:T(8,128)}, f32[1,48,384]{2,1,0:T(8,128)S(1)}, u32[]{:S(2)}) %copy-start.6) | copy-done | bytes 73752
  25.0 5.1 %join.1 = (f32[1,128,1024]{2,1,0:T(8,128)}, f32[1,128]{1,0:T(1,128)}) custom-call(f32[1,48,384]{2,1,0:T(8,128)} %get-tuple-element.5.refs_0_, f32[1,48,384]{2,1,0:T(8,128)} %copy-done.6, f32[1,48,384]{2,1,0:T(8,128)} %copy-done.5, f32[1,48,384]{2,1,0:T(8,128)} %copy-done.4, f32[1,48,384]{2,1,0:T(8,128)} %copy-done.3, f32[1,48,384]{2,1,0:T(8,128)} %copy-done.2, ...), custom_call_target="tpu_custom_call" | custom-call | tf_op jit(solution)/shard_map/join/pallas_call | solution.py:163
  (7 shorter events, 0.0 us)
Async XLA Ops:
  5.7 7.3 %collective-permute-start.6 = (f32[1,48,384]{2,1,0:T(8,128)}, f32[1,48,384]{2,1,0:T(8,128)S(1)}, u32[]{:S(2)}, u32[]{:S(2)}) collective-permute-start(f32[1,48,384]{2,1,0:T(8,128)} %get-tuple-element.5.refs_0_), channel_id=1, source_target_pairs={{28,0},{0,4},{4,8},{8,12},{12,16},{16,20},{20,24},{24,28},{29,1},{... | collective-permute-start | bytes 221192 | tf_op jit(solution)/shard_map/ppermute | solution.py:160
  7.2 11.7 %collective-permute-start.5 = (f32[1,48,384]{2,1,0:T(8,128)}, f32[1,48,384]{2,1,0:T(8,128)S(1)}, u32[]{:S(2)}, u32[]{:S(2)}) collective-permute-start(f32[1,48,384]{2,1,0:T(8,128)} %get-tuple-element.5.refs_0_), channel_id=1, source_target_pairs={{24,0},{28,4},{0,8},{4,12},{8,16},{12,20},{16,24},{20,28},{25,1},{... | collective-permute-start | bytes 221192 | tf_op jit(solution)/shard_map/ppermute | solution.py:160
  7.5 11.5 %collective-permute-start.4 = (f32[1,48,384]{2,1,0:T(8,128)}, f32[1,48,384]{2,1,0:T(8,128)S(1)}, u32[]{:S(2)}, u32[]{:S(2)}) collective-permute-start(f32[1,48,384]{2,1,0:T(8,128)} %get-tuple-element.5.refs_0_), channel_id=1, source_target_pairs={{20,0},{24,4},{28,8},{0,12},{4,16},{8,20},{12,24},{16,28},{21,1},{... | collective-permute-start | bytes 221192 | tf_op jit(solution)/shard_map/ppermute | solution.py:160
  9.1 9.9 %collective-permute-start.3 = (f32[1,48,384]{2,1,0:T(8,128)}, f32[1,48,384]{2,1,0:T(8,128)S(1)}, u32[]{:S(2)}, u32[]{:S(2)}) collective-permute-start(f32[1,48,384]{2,1,0:T(8,128)} %get-tuple-element.5.refs_0_), channel_id=1, source_target_pairs={{16,0},{20,4},{24,8},{28,12},{0,16},{4,20},{8,24},{12,28},{17,1},{... | collective-permute-start | bytes 221192 | tf_op jit(solution)/shard_map/ppermute | solution.py:160
  11.7 7.3 %collective-permute-start.2 = (f32[1,48,384]{2,1,0:T(8,128)}, f32[1,48,384]{2,1,0:T(8,128)S(1)}, u32[]{:S(2)}, u32[]{:S(2)}) collective-permute-start(f32[1,48,384]{2,1,0:T(8,128)} %get-tuple-element.5.refs_0_), channel_id=1, source_target_pairs={{12,0},{16,4},{20,8},{24,12},{28,16},{0,20},{4,24},{8,28},{13,1},{... | collective-permute-start | bytes 221192 | tf_op jit(solution)/shard_map/ppermute | solution.py:160
  13.0 11.4 %copy-start = (f32[1,48,384]{2,1,0:T(8,128)}, f32[1,48,384]{2,1,0:T(8,128)S(1)}, u32[]{:S(2)}) copy-start(f32[1,48,384]{2,1,0:T(8,128)S(1)} %collective-permute-done.6.refs_7_) | copy-start | bytes 221188
  13.0 7.2 %collective-permute-start.1 = (f32[1,48,384]{2,1,0:T(8,128)}, f32[1,48,384]{2,1,0:T(8,128)S(1)}, u32[]{:S(2)}, u32[]{:S(2)}) collective-permute-start(f32[1,48,384]{2,1,0:T(8,128)} %get-tuple-element.5.refs_0_), channel_id=1, source_target_pairs={{8,0},{12,4},{16,8},{20,12},{24,16},{28,20},{0,24},{4,28},{9,1},{1... | collective-permute-start | bytes 221192 | tf_op jit(solution)/shard_map/ppermute | solution.py:160
  18.9 5.5 %copy-start.1 = (f32[1,48,384]{2,1,0:T(8,128)}, f32[1,48,384]{2,1,0:T(8,128)S(1)}, u32[]{:S(2)}) copy-start(f32[1,48,384]{2,1,0:T(8,128)S(1)} %collective-permute-done.5.refs_6_) | copy-start | bytes 221188
  18.9 5.5 %collective-permute-start = (f32[1,48,384]{2,1,0:T(8,128)}, f32[1,48,384]{2,1,0:T(8,128)S(1)}, u32[]{:S(2)}, u32[]{:S(2)}) collective-permute-start(f32[1,48,384]{2,1,0:T(8,128)} %get-tuple-element.5.refs_0_), channel_id=1, source_target_pairs={{4,0},{8,4},{12,8},{16,12},{20,16},{24,20},{28,24},{0,28},{5,1},{9... | collective-permute-start | bytes 221192 | tf_op jit(solution)/shard_map/ppermute | solution.py:160
  18.9 5.5 %copy-start.2 = (f32[1,48,384]{2,1,0:T(8,128)}, f32[1,48,384]{2,1,0:T(8,128)S(1)}, u32[]{:S(2)}) copy-start(f32[1,48,384]{2,1,0:T(8,128)S(1)} %collective-permute-done.4.refs_5_) | copy-start | bytes 221188
  18.9 5.4 %copy-start.3 = (f32[1,48,384]{2,1,0:T(8,128)}, f32[1,48,384]{2,1,0:T(8,128)S(1)}, u32[]{:S(2)}) copy-start(f32[1,48,384]{2,1,0:T(8,128)S(1)} %collective-permute-done.3.refs_4_) | copy-start | bytes 221188
  19.0 5.4 %copy-start.4 = (f32[1,48,384]{2,1,0:T(8,128)}, f32[1,48,384]{2,1,0:T(8,128)S(1)}, u32[]{:S(2)}) copy-start(f32[1,48,384]{2,1,0:T(8,128)S(1)} %collective-permute-done.2.refs_3_) | copy-start | bytes 221188
  20.2 4.2 %copy-start.5 = (f32[1,48,384]{2,1,0:T(8,128)}, f32[1,48,384]{2,1,0:T(8,128)S(1)}, u32[]{:S(2)}) copy-start(f32[1,48,384]{2,1,0:T(8,128)S(1)} %collective-permute-done.1.refs_2_) | copy-start | bytes 221188
  24.4 0.6 %copy-start.6 = (f32[1,48,384]{2,1,0:T(8,128)}, f32[1,48,384]{2,1,0:T(8,128)S(1)}, u32[]{:S(2)}) copy-start(f32[1,48,384]{2,1,0:T(8,128)S(1)} %collective-permute-done.refs_1_) | copy-start | bytes 221188

commit v2 on v1

v2 whole, which is shorter than its diff:
```python
import functools

import jax
import jax.numpy as jnp
from jax import lax
from jax.experimental import pallas as pl
from jax.experimental.pallas import tpu as pltpu
from jax.sharding import PartitionSpec as P

LANES = 128
HALF = 64


def split(x):
    high = x.astype(jnp.bfloat16)
    return high, (x - high.astype(jnp.float32)).astype(jnp.bfloat16)


def product(left, right, form="nn"):
    dims = (((0 if form[0] == "t" else 1,), (1 if form[1] == "t" else 0,)), ((), ()))
    mul = functools.partial(
        lax.dot_general, dimension_numbers=dims, preferred_element_type=jnp.float32
    )
    (lh, ll), (rh, rl) = split(left), split(right)
    return mul(lh, rh) + (mul(lh, rl) + mul(ll, rh))


def iota(shape, dim):
    return lax.broadcasted_iota(jnp.int32, shape, dim)


def respond(first, last, start):
    if last - first == 1:
        return [start[first]]
    middle = (first + last) // 2
    left, right = respond(first, middle, start), respond(middle, last, start)
    nx, width = left[0].shape
    cols = width - LANES
    maps = [x[:, cols : cols + nx] for x in right]
    through = product(jnp.concatenate(maps, 0), left[-1])
    lane = iota((nx, width), 1)
    keep = (lane < cols) | (lane >= cols + nx)
    return left + [
        through[i * nx : (i + 1) * nx] + jnp.where(keep, x, 0.0) for i, x in enumerate(right)
    ]


def local_kernel(*refs):
    sources, (pay_ref, own_ref, side_ref, state_ref) = refs[:7], refs[7:11]
    held, sem = refs[11:18], refs[18]
    copies = [
        pltpu.make_async_copy(source, target, sem.at[i])
        for i, (source, target) in enumerate(zip(sources, held))
    ]
    for copy in copies:
        copy.start()
    for copy in copies:
        copy.wait()
    a_ref, b_ref, f_ref, q_ref, g_ref, r_ref, x_ref = held
    problems, sections, nu, nx = b_ref.shape
    cols = sections * nu
    for p in range(problems):
        controls = b_ref[p].reshape(cols, nx).T
        drift = f_ref[p].T
        target = g_ref[p].T
        pad = jnp.zeros((nx, LANES - nx - 1), jnp.float32)
        section = iota((nx, cols), 1) // nu
        start = [
            jnp.concatenate(
                [
                    jnp.where(section == s, controls, 0.0),
                    jnp.concatenate([a_ref[p, s], drift[:, s : s + 1], pad], 1),
                ],
                1,
            )
            for s in range(sections)
        ]
        states = respond(0, sections, start)
        lane = iota((nx, cols + LANES), 1)
        errors = [
            jnp.where(lane == cols + nx, x - target[:, s : s + 1], x)
            for s, x in enumerate(states)
        ]
        weighted = [product(q_ref[p, s], e) for s, e in enumerate(errors)]
        square = product(jnp.concatenate(errors, 0), jnp.concatenate(weighted, 0), "tn")
        costs = r_ref[p].reshape(cols, nu)
        copies = (iota((nu, cols), 1) % nu == iota((nu, cols), 0)).astype(jnp.float32)
        same = iota((cols, cols), 0) // nu == iota((cols, cols), 1) // nu
        own_ref[p] = square[:cols, :cols] + jnp.where(same, product(costs, copies), 0.0)
        side_ref[p] = square[:cols, cols : cols + LANES]
        ones = jnp.ones((1, 1), jnp.float32)
        pad = jnp.zeros((1, LANES - nx - 1), jnp.float32)
        state_ref[p] = jnp.concatenate([x_ref[pl.ds(p, 1), :], ones, pad], 1)
        end = states[-1]
        pay_ref[p, :, :cols] = end[:, :cols]
        pay_ref[p, :, cols : cols + LANES] = jnp.concatenate(
            [end[:, cols : cols + HALF], square[cols : cols + nx, cols : cols + HALF]], 1
        )
        pay_ref[p, :, cols + LANES :] = square[cols : cols + nx, :cols]


def join_kernel(outer, inner, *refs):
    count = outer * inner
    pays, (own_ref, side_ref, x_ref, h_ref, grad_ref) = refs[:count], refs[count:]
    nx = pays[0].shape[1]
    device = lax.axis_index("horizon")
    place = lax.rem(device, inner)
    problems, cols, _ = own_ref.shape
    upper = [device + k < count for k in range(count)]
    for p in range(problems):

        def block(k):
            step, turn = k // inner, k % inner
            here = pays[step * inner + turn][p]
            if not turn:
                return here
            return jnp.where(
                place + turn >= inner, pays[(step + 1) % outer * inner + turn][p], here
            )

        blocks = [block(k) for k in range(count)]
        last = lambda x: jnp.where(iota(x.shape, 1) == nx, x, 0.0)
        moved = [None, blocks[0][:, :cols].T]
        sent = [None]
        for k in range(1, count):
            moved[k] = jnp.where(upper[k], moved[k], 0.0)
            sent.append(product(moved[k], blocks[k][:, cols:]))
            if k + 1 < count:
                moved.append(product(moved[k], blocks[k][:, cols : cols + nx], "nt"))
        carried = blocks[-1][:, cols : cols + HALF]
        entry = [None] * count
        entry[-1] = blocks[-1][:, :cols]
        eye = (iota((nx, HALF), 0) == iota((nx, HALF), 1)).astype(jnp.float32)
        carried = jnp.where(upper[-1], eye, carried)
        for k in reversed(range(1, count - 1)):
            step = product(carried[:, :nx], blocks[k][:, : cols + LANES])
            entry[k] = step[:, :cols]
            carried = jnp.where(
                upper[k], carried, step[:, cols : cols + HALF] + last(carried)
            )
        costate = sent[-1][:, HALF:LANES]
        tiles = [None] * count
        tiles[-1] = sent[-1][:, LANES:]
        for k in reversed(range(count - 1)):
            back = product(costate[:, :nx], blocks[k][:, : cols + LANES])
            if k:
                tiles[k] = sent[k][:, LANES:] + back[:, :cols]
                more = sent[k][:, HALF:LANES]
            else:
                tiles[k] = own_ref[p] + back[:, :cols]
                more = side_ref[p, :, :HALF]
            costate = back[:, cols : cols + HALF] + more + last(costate)
        for k in range(count):
            tile = tiles[k]
            if k:
                tile = jnp.where(upper[k], tile, product(costate[:, :nx], entry[k]))
            at = pl.multiple_of(lax.rem(device + k, count) * cols, cols)
            h_ref[p, :, pl.ds(at, cols)] = tile
        ones = jnp.ones((1, 1), jnp.float32)
        pad = jnp.zeros((1, HALF - nx - 1), jnp.float32)
        state = product(x_ref[p, :, :HALF], carried, "nt")
        state = jnp.concatenate([state, ones, pad], 1)
        grad_ref[pl.ds(p, 1), :] = product(state, costate, "nt")


def gather(block, count, inner):
    outer = count // inner
    sets = [[block]]
    for i in range(1, outer):
        pairs = [((d + i * inner) % count, d) for d in range(count)]
        sets.append([lax.ppermute(block, "horizon", pairs)])
    for group in sets:
        for j in range(1, inner):
            pairs = [(d // inner * inner + (d + j) % inner, d) for d in range(count)]
            group.append(lax.ppermute(group[0], "horizon", pairs))
    return [block for group in sets for block in group]


def body(dynamics, inputs, state_cost, input_cost, drift, target, initial):
    count = lax.axis_size("horizon")
    inner = 1
    while inner * inner * 4 <= count and count % (inner * 2) == 0:
        inner *= 2
    problems, sections, nx, nu = inputs.shape
    cols = sections * nu
    f32 = jnp.float32
    turned = jnp.swapaxes(inputs, 2, 3)
    operands = (dynamics, turned, drift, state_cost, target, input_cost, initial)
    operands = [pltpu.with_memory_space_constraint(x, pltpu.HBM) for x in operands]
    pay, own, side, state = pl.pallas_call(
        local_kernel,
        out_shape=(
            jax.ShapeDtypeStruct((problems, nx, 2 * cols + LANES), f32),
            jax.ShapeDtypeStruct((problems, cols, cols), f32),
            jax.ShapeDtypeStruct((problems, cols, LANES), f32),
            jax.ShapeDtypeStruct((problems, 1, LANES), f32),
        ),
        in_specs=[pl.BlockSpec(memory_space=pltpu.HBM)] * len(operands),
        scratch_shapes=[pltpu.VMEM(x.shape, x.dtype) for x in operands]
        + [pltpu.SemaphoreType.DMA((len(operands),))],
        compiler_params=pltpu.CompilerParams(vmem_limit_bytes=16 << 20),
        name="local",
    )(*operands)
    pays = gather(pay, count, inner)
    return pl.pallas_call(
        functools.partial(join_kernel, count // inner, inner),
        out_shape=(
            jax.ShapeDtypeStruct((problems, cols, count * cols), f32),
            jax.ShapeDtypeStruct((problems, cols), f32),
        ),
        compiler_params=pltpu.CompilerParams(vmem_limit_bytes=16 << 20),
        name="join",
    )(*pays, own, side, state)


def solution(mesh):
    in_specs = (
        P("batch", "horizon", None, None),
        P("batch", "horizon", None, None),
        P("batch", "horizon", None, None),
        P("batch", "horizon", None, None),
        P("batch", "horizon", None),
        P("batch", "horizon", None),
        P("batch", None),
    )
    out_specs = (P("batch", "horizon", None), P("batch", "horizon"))
    return jax.shard_map(body, mesh=mesh, in_specs=in_specs, out_specs=out_specs, check_vma=False)
```

time: 30.4 us -> 24.5 us (0.81)
  the two profiles are of different devices: /device:TPU:22 before, /device:TPU:0 now
where the time goes in v2:
time: 24.5 us; the launch traced here: 24.3 us
  starting transfers between devices  11.7 us (48%)
  Pallas kernels  6.98 us (28%)
  waiting for transfers between devices  4.98 us (20%)
  between operations  0.65 us (3%)
    ppermute x3, starting transfers between devices, gather(): sets.append([lax.ppermute(block, 'horizon', pairs)])  7.04 us
    ppermute x4, starting transfers between devices, gather(): group.append(lax.ppermute(group[0], 'horizon', pairs))  4.67 us
    pallas_call x1, Pallas kernels, body(): pl.pallas_call(functools.partial(join_kernel, count // inner, inner), out...  4.39 us
    ppermute x4, waiting for transfers between devices, gather(): group.append(lax.ppermute(group[0], 'horizon', pairs))  4 us
    pallas_call x1, Pallas kernels, body(): pl.pallas_call(local_kernel, out_shape=(jax.ShapeDtypeStruct((problems, n...  2.6 us
    ppermute x3, waiting for transfers between devices, gather(): sets.append([lax.ppermute(block, 'horizon', pairs)])  0.97 us
  transfers between devices with their start and end apart: 7, of which 4 were waited for; matrix products, arithmetic and copies ran while one was open for 0% of the time, Pallas kernels for 0%

profile of v2, /device:TPU:0, one launch (start us, length us, event | category | flops | bytes accessed | tf_op | source)
XLA Modules:
  0.0 24.3 jit_solution(3479160183581927299)
XLA Ops:
  0.6 2.6 %local.1 = (f32[1,48,384]{2,1,0:T(8,128)S(1)}, f32[1,128,128]{2,1,0:T(8,128)S(1)}, f32[1,128,128]{2,1,0:T(8,128)S(1)}, f32[1,1,128]{2,1,0:T(1,128)S(1)}) custom-call(f32[1,8,48,48]{3,2,1,0:T(8,128)} %refs_0_.1, f32[1,8,16,48]{3,2,1,0:T(8,128)} %bitcast.1, f32[1,8,48]{2,1,0:T(8,128)} %refs_2_.1, f32[1,8,48,48]{3,2,1,0:T(8,128)} %refs_3_.1, ...), custom_call_target="tpu_custom_call" | custom-call | tf_op jit(solution)/shard_map/local/pallas_call | solution.py:190
  3.2 3.1 %collective-permute-start.5 = (f32[1,48,384]{2,1,0:T(8,128)S(1)}, f32[1,48,384]{2,1,0:T(8,128)S(1)}, u32[]{:S(2)}, u32[]{:S(2)}) collective-permute-start(f32[1,48,384]{2,1,0:T(8,128)S(1)} %get-tuple-element.6.refs_0_), channel_id=1, source_target_pairs={{24,0},{28,4},{0,8},{4,12},{8,16},{12,20},{16,24},{20,28},{25,1},{... | collective-permute-start | bytes 221192 | tf_op jit(solution)/shard_map/ppermute | solution.py:171
  6.3 2.6 %collective-permute-start.3 = (f32[1,48,384]{2,1,0:T(8,128)S(1)}, f32[1,48,384]{2,1,0:T(8,128)S(1)}, u32[]{:S(2)}, u32[]{:S(2)}) collective-permute-start(f32[1,48,384]{2,1,0:T(8,128)S(1)} %get-tuple-element.6.refs_0_), channel_id=1, source_target_pairs={{16,0},{20,4},{24,8},{28,12},{0,16},{4,20},{8,24},{12,28},{17,1},{... | collective-permute-start | bytes 221192 | tf_op jit(solution)/shard_map/ppermute | solution.py:171
  8.9 1.4 %collective-permute-start.1 = (f32[1,48,384]{2,1,0:T(8,128)S(1)}, f32[1,48,384]{2,1,0:T(8,128)S(1)}, u32[]{:S(2)}, u32[]{:S(2)}) collective-permute-start(f32[1,48,384]{2,1,0:T(8,128)S(1)} %get-tuple-element.6.refs_0_), channel_id=1, source_target_pairs={{8,0},{12,4},{16,8},{20,12},{24,16},{28,20},{0,24},{4,28},{9,1},{1... | collective-permute-start | bytes 221192 | tf_op jit(solution)/shard_map/ppermute | solution.py:171
  10.3 1.5 %collective-permute-start = (f32[1,48,384]{2,1,0:T(8,128)S(1)}, f32[1,48,384]{2,1,0:T(8,128)S(1)}, u32[]{:S(2)}, u32[]{:S(2)}) collective-permute-start(f32[1,48,384]{2,1,0:T(8,128)S(1)} %get-tuple-element.6.refs_0_), channel_id=1, source_target_pairs={{4,0},{0,4},{12,8},{8,12},{20,16},{16,20},{28,24},{24,28},{5,1},{1... | collective-permute-start | bytes 221192 | tf_op jit(solution)/shard_map/ppermute | solution.py:175
  11.8 0.0 collective-permute-done.5.refs_6_
  11.8 1.1 %collective-permute-start.6 = (f32[1,48,384]{2,1,0:T(8,128)S(1)}, f32[1,48,384]{2,1,0:T(8,128)S(1)}, u32[]{:S(2)}, u32[]{:S(2)}) collective-permute-start(f32[1,48,384]{2,1,0:T(8,128)S(1)} %collective-permute-done.5.refs_6_), channel_id=1, source_target_pairs={{4,0},{0,4},{12,8},{8,12},{20,16},{16,20},{28,24},{24,28},{5,1},{1... | collective-permute-start | bytes 221192 | tf_op jit(solution)/shard_map/ppermute | solution.py:175
  12.9 1.0 %collective-permute-done.3.refs_4_ = f32[1,48,384]{2,1,0:T(8,128)S(1)} collective-permute-done((f32[1,48,384]{2,1,0:T(8,128)S(1)}, f32[1,48,384]{2,1,0:T(8,128)S(1)}, u32[]{:S(2)}, u32[]{:S(2)}) %collective-permute-start.3) | collective-permute-done | bytes 73760 | tf_op jit(solution)/shard_map/ppermute | solution.py:171
  13.9 1.7 %collective-permute-start.4 = (f32[1,48,384]{2,1,0:T(8,128)S(1)}, f32[1,48,384]{2,1,0:T(8,128)S(1)}, u32[]{:S(2)}, u32[]{:S(2)}) collective-permute-start(f32[1,48,384]{2,1,0:T(8,128)S(1)} %collective-permute-done.3.refs_4_), channel_id=1, source_target_pairs={{4,0},{0,4},{12,8},{8,12},{20,16},{16,20},{28,24},{24,28},{5,1},{1... | collective-permute-start | bytes 221192 | tf_op jit(solution)/shard_map/ppermute | solution.py:175
  15.6 0.0 collective-permute-done.1.refs_2_
  15.6 0.4 %collective-permute-start.2 = (f32[1,48,384]{2,1,0:T(8,128)S(1)}, f32[1,48,384]{2,1,0:T(8,128)S(1)}, u32[]{:S(2)}, u32[]{:S(2)}) collective-permute-start(f32[1,48,384]{2,1,0:T(8,128)S(1)} %collective-permute-done.1.refs_2_), channel_id=1, source_target_pairs={{4,0},{0,4},{12,8},{8,12},{20,16},{16,20},{28,24},{24,28},{5,1},{1... | collective-permute-start | bytes 221192 | tf_op jit(solution)/shard_map/ppermute | solution.py:175
  15.9 0.0 collective-permute-done.refs_1_
  15.9 0.2 collective-permute-done.6.refs_7_
  16.1 2.9 %collective-permute-done.4.refs_5_ = f32[1,48,384]{2,1,0:T(8,128)S(1)} collective-permute-done((f32[1,48,384]{2,1,0:T(8,128)S(1)}, f32[1,48,384]{2,1,0:T(8,128)S(1)}, u32[]{:S(2)}, u32[]{:S(2)}) %collective-permute-start.4) | collective-permute-done | bytes 73760 | tf_op jit(solution)/shard_map/ppermute | solution.py:175
  19.0 0.9 %collective-permute-done.2.refs_3_ = f32[1,48,384]{2,1,0:T(8,128)S(1)} collective-permute-done((f32[1,48,384]{2,1,0:T(8,128)S(1)}, f32[1,48,384]{2,1,0:T(8,128)S(1)}, u32[]{:S(2)}, u32[]{:S(2)}) %collective-permute-start.2) | collective-permute-done | bytes 73760 | tf_op jit(solution)/shard_map/ppermute | solution.py:175
  19.9 4.4 %join.1 = (f32[1,128,1024]{2,1,0:T(8,128)}, f32[1,128]{1,0:T(1,128)}) custom-call(f32[1,48,384]{2,1,0:T(8,128)S(1)} %get-tuple-element.6.refs_0_, f32[1,48,384]{2,1,0:T(8,128)S(1)} %collective-permute-done.refs_1_, f32[1,48,384]{2,1,0:T(8,128)S(1)} %collective-permute-done.1.refs_2_, f32[1,48,384]{2,1,0:T(8,128)S(1)} %collective-permute-done.2.refs_3_, ...), custom_call_target="tpu_custom_call" | custom-call | tf_op jit(solution)/shard_map/join/pallas_call | solution.py:205
Async XLA Ops:
  3.2 8.5 %collective-permute-start.5 = (f32[1,48,384]{2,1,0:T(8,128)S(1)}, f32[1,48,384]{2,1,0:T(8,128)S(1)}, u32[]{:S(2)}, u32[]{:S(2)}) collective-permute-start(f32[1,48,384]{2,1,0:T(8,128)S(1)} %get-tuple-element.6.refs_0_), channel_id=1, source_target_pairs={{24,0},{28,4},{0,8},{4,12},{8,16},{12,20},{16,24},{20,28},{25,1},{... | collective-permute-start | bytes 221192 | tf_op jit(solution)/shard_map/ppermute | solution.py:171
  6.3 7.5 %collective-permute-start.3 = (f32[1,48,384]{2,1,0:T(8,128)S(1)}, f32[1,48,384]{2,1,0:T(8,128)S(1)}, u32[]{:S(2)}, u32[]{:S(2)}) collective-permute-start(f32[1,48,384]{2,1,0:T(8,128)S(1)} %get-tuple-element.6.refs_0_), channel_id=1, source_target_pairs={{16,0},{20,4},{24,8},{28,12},{0,16},{4,20},{8,24},{12,28},{17,1},{... | collective-permute-start | bytes 221192 | tf_op jit(solution)/shard_map/ppermute | solution.py:171
  8.9 6.6 %collective-permute-start.1 = (f32[1,48,384]{2,1,0:T(8,128)S(1)}, f32[1,48,384]{2,1,0:T(8,128)S(1)}, u32[]{:S(2)}, u32[]{:S(2)}) collective-permute-start(f32[1,48,384]{2,1,0:T(8,128)S(1)} %get-tuple-element.6.refs_0_), channel_id=1, source_target_pairs={{8,0},{12,4},{16,8},{20,12},{24,16},{28,20},{0,24},{4,28},{9,1},{1... | collective-permute-start | bytes 221192 | tf_op jit(solution)/shard_map/ppermute | solution.py:171
  10.3 5.6 %collective-permute-start = (f32[1,48,384]{2,1,0:T(8,128)S(1)}, f32[1,48,384]{2,1,0:T(8,128)S(1)}, u32[]{:S(2)}, u32[]{:S(2)}) collective-permute-start(f32[1,48,384]{2,1,0:T(8,128)S(1)} %get-tuple-element.6.refs_0_), channel_id=1, source_target_pairs={{4,0},{0,4},{12,8},{8,12},{20,16},{16,20},{28,24},{24,28},{5,1},{1... | collective-permute-start | bytes 221192 | tf_op jit(solution)/shard_map/ppermute | solution.py:175
  11.8 4.4 %collective-permute-start.6 = (f32[1,48,384]{2,1,0:T(8,128)S(1)}, f32[1,48,384]{2,1,0:T(8,128)S(1)}, u32[]{:S(2)}, u32[]{:S(2)}) collective-permute-start(f32[1,48,384]{2,1,0:T(8,128)S(1)} %collective-permute-done.5.refs_6_), channel_id=1, source_target_pairs={{4,0},{0,4},{12,8},{8,12},{20,16},{16,20},{28,24},{24,28},{5,1},{1... | collective-permute-start | bytes 221192 | tf_op jit(solution)/shard_map/ppermute | solution.py:175
  13.9 5.1 %collective-permute-start.4 = (f32[1,48,384]{2,1,0:T(8,128)S(1)}, f32[1,48,384]{2,1,0:T(8,128)S(1)}, u32[]{:S(2)}, u32[]{:S(2)}) collective-permute-start(f32[1,48,384]{2,1,0:T(8,128)S(1)} %collective-permute-done.3.refs_4_), channel_id=1, source_target_pairs={{4,0},{0,4},{12,8},{8,12},{20,16},{16,20},{28,24},{24,28},{5,1},{1... | collective-permute-start | bytes 221192 | tf_op jit(solution)/shard_map/ppermute | solution.py:175
  15.6 4.4 %collective-permute-start.2 = (f32[1,48,384]{2,1,0:T(8,128)S(1)}, f32[1,48,384]{2,1,0:T(8,128)S(1)}, u32[]{:S(2)}, u32[]{:S(2)}) collective-permute-start(f32[1,48,384]{2,1,0:T(8,128)S(1)} %collective-permute-done.1.refs_2_), channel_id=1, source_target_pairs={{4,0},{0,4},{12,8},{8,12},{20,16},{16,20},{28,24},{24,28},{5,1},{1... | collective-permute-start | bytes 221192 | tf_op jit(solution)/shard_map/ppermute | solution.py:175
